TPU v7x, 128 devices: a whole 4x4x4 slice. The times are simulated.
128 devices in a mesh: dom: 128 (over z, y, x, core).
Axes of the slice: x: 4, y: 4, z: 4, core: 2. Of those that a mesh axis runs over, the one named last changes fastest.
Arguments:
- features: bfloat16 [131072, 256], P('dom'), may hold values from -6 to 6
- edge_source: int32 [128, 128, 128], P('dom'), may hold values from 0 to 5119, as said below
- edge_relation: int32 [128, 128, 128], P('dom'), may hold values from 0 to 7
- edge_target: int32 [128, 128, 128], P('dom'), may hold values from 0 to 1023, as said below
- block_count: int32 [128], P('dom'), may hold values from 1 to 128, as said below
- send_list: int32 [128, 128, 32], P('dom'), may hold values from 0 to 1023
- bases_first: bfloat16 [30, 256, 256], P(None, 'dom'), may hold values from -0.375 to 0.375
- self_first: bfloat16 [256, 256], P('dom'), may hold values from -0.375 to 0.375
- coef_first: float32 [8, 30], replicated, may hold values from -1 to 1
- bias_first: float32 [256], replicated, may hold values from -3 to 3
- bases_second: bfloat16 [30, 256, 256], P(None, 'dom'), may hold values from -0.375 to 0.375
- self_second: bfloat16 [256, 256], P('dom'), may hold values from -0.375 to 0.375
- coef_second: float32 [8, 30], replicated, may hold values from -1 to 1
- bias_second: float32 [256], replicated, may hold values from -3 to 3
Outputs:
- embedded: bfloat16 [131072, 256], P('dom')
Inputs may be any that keep to these rules, and one draw needn't show every extreme that they name: `edge_source`: an entry below 1024 names a row of the edge's own partition; an entry 1024 + p * 32 + s names the row that partition p sends to the edge's partition in slot s, and p is never the edge's own partition. `edge_target`: non-decreasing within each block; all targets of one block lie in one aligned window of 16 rows, from 16 * k to 16 * k + 15 for some k. `block_count`: blocks at and beyond it are ignored; some partition uses all 128.
All inputs are finite; a program needn't handle non-finite values.
Results may differ from a plain program's by a relative error of at most 0.0064.
Values may be sent and summed in bfloat16 or wider, within the bound.
A program may use at most 128 MiB of HBM per device.

v0:
```python
import functools

import jax
import jax.numpy as jnp
from jax import lax
from jax.experimental import pallas as pl
from jax.experimental.pallas import tpu as pltpu
from jax.sharding import PartitionSpec as P

WIN = 16
LANES = 128
VMEM = pl.BlockSpec(memory_space=pltpu.VMEM)
SMEM = pl.BlockSpec(memory_space=pltpu.SMEM)
LIMIT = 60 * 1024 * 1024


def mix_weights(layer, coef_ref, bases_ref, self_ref, part_ref):
    relations = coef_ref.shape[0]
    rows = []
    for i in range(2):
        bases = bases_ref[:, i, :].astype(jnp.float32)
        rows.append(
            jnp.dot(
                coef_ref[...],
                bases,
                precision=lax.Precision.HIGHEST,
                preferred_element_type=jnp.float32,
            )
        )
    for h in range(2):
        lanes = slice(h * LANES, (h + 1) * LANES)
        for r in range(relations):
            both = jnp.concatenate([row[r : r + 1, lanes] for row in rows], axis=0)
            part_ref[layer, r, h] = both.astype(jnp.bfloat16)
        part_ref[layer, relations, h] = self_ref[:, lanes]


MESH = pl.DeviceIdType.MESH
ANY = pl.BlockSpec(memory_space=pl.ANY)
GROUP = 8
FIRST_GROUPS = 6
CHUNK_BLOCKS = 8


def rows_of_group(group, send_ref, rows_ref, out_ref):
    slots = send_ref.shape[1]
    nodes, width = rows_ref.shape
    ids = send_ref[pl.ds(pl.multiple_of(group * GROUP, GROUP), GROUP), :]
    hot = (
        (ids[:, :, None] == lax.broadcasted_iota(jnp.int32, (GROUP, slots, nodes), 2))
        .astype(jnp.float32)
        .astype(jnp.bfloat16)
        .reshape(GROUP * slots, nodes)
    )
    got = jnp.dot(hot, rows_ref[...], preferred_element_type=jnp.float32)
    out_ref[pl.ds(group * GROUP, GROUP)] = got.astype(jnp.bfloat16).reshape(GROUP, slots, width)


def remote(src, dst, send_sem, recv_sem, to):
    return pltpu.make_async_remote_copy(
        src_ref=src,
        dst_ref=dst,
        send_sem=send_sem,
        recv_sem=recv_sem,
        device_id=(to,),
        device_id_type=MESH,
    )


def tally_slots(target_ref, relation_ref, tally_ref):
    blocks, block_width = target_ref.shape
    slots = tally_ref.shape[1]
    lane = lax.broadcasted_iota(jnp.int32, (8, 2 * block_width), 1) // block_width
    row = lax.broadcasted_iota(jnp.int32, (8, 2 * block_width), 0)
    slot_ids = lax.broadcasted_iota(jnp.int32, (slots, 2 * block_width), 0)

    def tally(g, carry):
        at = pl.ds(pl.multiple_of(8 * g, 8), 8)
        slot = relation_ref[at, :] * WIN + lax.bitwise_and(target_ref[at, :], WIN - 1)
        total = jnp.zeros((8, slots), jnp.float32)
        for p in range(4):
            both = jnp.concatenate([slot[2 * p : 2 * p + 1], slot[2 * p + 1 : 2 * p + 2]], axis=1)
            hot = (both == slot_ids).astype(jnp.float32).astype(jnp.bfloat16)
            pick = (row == lane + 2 * p).astype(jnp.float32).astype(jnp.bfloat16)
            total = total + lax.dot_general(
                pick, hot, (((1,), (1,)), ((), ())), preferred_element_type=jnp.float32
            )
        tally_ref[at, :] = total
        return carry

    lax.fori_loop(0, blocks // 8, tally, 0)


def invert_degrees(count_ref, target_ref, tally_ref, windows):
    blocks = target_ref.shape[0]
    window = lax.shift_right_logical(target_ref[...].T[:1, :], 4)
    in_use = lax.broadcasted_iota(jnp.int32, (windows, blocks), 1) < count_ref[0]
    same = window == lax.broadcasted_iota(jnp.int32, (windows, blocks), 0)
    held = jnp.logical_and(same, in_use).astype(jnp.float32).astype(jnp.bfloat16)
    degree = jnp.dot(
        held, tally_ref[...].astype(jnp.bfloat16), preferred_element_type=jnp.float32
    )
    tally_ref[:windows, :] = 1.0 / jnp.maximum(degree, 1.0)


def spread_windows(first, last, tally_ref, inverse_ref):
    slots = tally_ref.shape[1]

    def spread(w, carry):
        row = jnp.broadcast_to(tally_ref[pl.ds(w, 1), :], (slots, slots))
        inverse_ref[pl.ds(pl.multiple_of(w * slots, slots), slots), :] = row.T
        return carry

    lax.fori_loop(first, last, spread, 0)


def exchange_body(count, with_weights, *refs):
    if with_weights:
        (turned_ref, rows_ref, coef_a, bases_a, self_a, coef_b, bases_b, self_b,
         count_ref, target_ref, relation_ref,
         in_ref, full_ref, inverse_out, out_ref, send_ref, part_ref, tally_ref, inverse_ref,
         send_sem, recv_sem, plane_send, plane_recv, far_send, far_recv, core_send, core_recv,
         inverse_sem) = refs
    else:
        turned_ref, rows_ref, in_ref, out_ref, send_ref, send_sem, recv_sem = refs
    me = lax.axis_index("dom")
    groups = count // GROUP
    barrier = pltpu.get_barrier_semaphore()

    for k in range(1, count):
        pl.semaphore_signal(
            barrier, inc=1, device_id=(lax.rem(me + k, count),), device_id_type=MESH
        )

    def group_at(t):
        return lax.rem(me // GROUP + 5 * t, groups)

    def compute(t):
        rows_of_group(group_at(t), send_ref, rows_ref, out_ref)

    def send(t, first):
        for i in range(first, GROUP):
            to = group_at(t) * GROUP + lax.rem(me + i, GROUP)
            remote(out_ref.at[to], in_ref.at[me], send_sem, recv_sem, to).start()

    def step(t, carry):
        compute(t + 1)
        send(t, 0)
        return carry

    send_ref[...] = turned_ref[...].T
    if with_weights:
        mix_weights(0, coef_a, bases_a, self_a, part_ref)
        mix_weights(1, coef_b, bases_b, self_b, part_ref)
    compute(0)
    compute(1)
    pl.semaphore_wait(barrier, count - 1)
    if with_weights:
        core = lax.rem(me, 2)
        x = lax.rem(me // 2, 4)
        y = lax.rem(me // 8, 4)
        z = me // 32
        pair = lax.rem(me, 8)
        mine = pltpu.make_async_copy(
            part_ref.at[core], full_ref.at[core, :, :, z, y, pair], plane_recv
        )
        mine.start()

        def spread(layer):
            def one(k, carry):
                column = lax.rem(x + k, 4)
                if layer == 0:
                    line = (z * 4 + lax.rem(y + k // 4, 4)) * 4
                else:
                    line = (lax.rem(z + k // 4, 4) * 4 + y) * 4
                remote(
                    part_ref.at[layer],
                    full_ref.at[layer, :, :, z, y, pair],
                    plane_send.at[jnp.where(core == layer, 0, 1)],
                    plane_recv,
                    (line + column) * 2 + layer,
                ).start()
                return carry

            lax.fori_loop(jnp.where(core == layer, 1, 0), 16, one, 0)

        spread(0)
        spread(1)
    send(0, 1)
    if not with_weights:
        lax.fori_loop(1, groups - 1, step, 0)
    else:
        lax.fori_loop(1, FIRST_GROUPS, step, 0)
        arrived = full_ref.at[0, :, :, 0]
        pltpu.make_async_copy(arrived, arrived, plane_recv).wait()

        def slab_of(layer, back):
            if layer == 0:
                return full_ref.at[0, :, :, lax.rem(z + 4 - back, 4)]
            return full_ref.at[1, :, :, :, lax.rem(y + 4 - back, 4)]

        def far(layer, k):
            slab = slab_of(layer, 0)
            if layer == 0:
                to = lax.rem(me + 32 * k, count)
            else:
                to = z * 32 + lax.rem(y + k, 4) * 8 + pair
            return remote(slab, slab, far_send.at[k], far_recv.at[k], to)

        def across(layer, k):
            slab = slab_of(layer, k)
            return remote(slab, slab, core_send.at[k], core_recv.at[k], me + 1 - 2 * core)

        for layer in range(2):
            @pl.when(core == layer)
            def _():
                for k in (1, 3, 2):
                    far(layer, k).start()
                across(layer, 0).start()

        lax.fori_loop(FIRST_GROUPS, groups - 1, step, 0)
    send(groups - 1, 0)
    if with_weights:
        tally_slots(target_ref, relation_ref, tally_ref)
        slots = tally_ref.shape[1]
        windows = inverse_ref.shape[0] // slots
        quarter = windows // 4
        invert_degrees(count_ref, target_ref, tally_ref, windows)

        def put(q):
            rows = pl.ds(q * quarter * slots, quarter * slots)
            return pltpu.make_async_copy(
                inverse_ref.at[rows], inverse_out.at[rows], inverse_sem.at[q]
            )

        for q in range(4):
            spread_windows(q * quarter, (q + 1) * quarter, tally_ref, inverse_ref)
            if q > 0:
                put(q - 1).start()
        for layer in range(2):
            @pl.when(core == layer)
            def _():
                for k in (1, 3, 2):
                    far(layer, k).wait_recv()
                    across(layer, k).start()
        for layer in range(2):
            @pl.when(core == layer)
            def _():
                for k in (1, 3, 2):
                    far(layer, k).wait_send()
                for k in (0, 1, 3, 2):
                    across(layer, k).wait()
        put(3).start()
        for q in range(4):
            put(q).wait()
        gone = full_ref.at[0, :, :, 0:3, 0, 0:5]
        pltpu.make_async_copy(gone, gone, plane_send.at[0]).wait()
        gone = full_ref.at[0, :, :, 0:2, 0]
        pltpu.make_async_copy(gone, gone, plane_send.at[1]).wait()
    some = pl.ds(0, count - 1)
    pltpu.make_async_copy(in_ref.at[some], in_ref.at[some], recv_sem).wait()
    pltpu.make_async_copy(out_ref.at[some], out_ref.at[some], send_sem).wait()


def exchange(turned, rows, weights=(), edges=()):
    slots, count = turned.shape
    block = (count, slots, rows.shape[1])
    out_shape = [jax.ShapeDtypeStruct(block, rows.dtype)]
    scratch = [pltpu.VMEM(block, rows.dtype), pltpu.VMEM((count, slots), turned.dtype)]
    sems = [pltpu.SemaphoreType.DMA] * 2
    if weights:
        matrices = weights[0].shape[0] + 1
        halves = rows.shape[1] // LANES
        out_shape.append(
            jax.ShapeDtypeStruct((2, matrices, halves, 4, 4, 8, 2, LANES), rows.dtype)
        )
        slots = (matrices - 1) * WIN
        scratch.append(pltpu.VMEM((2, matrices, halves, 2, LANES), rows.dtype))
        scratch.append(pltpu.VMEM((edges[1].shape[0], slots), jnp.float32))
        inverse = (rows.shape[0] * (matrices - 1), LANES)
        scratch.append(pltpu.VMEM(inverse, jnp.float32))
        out_shape.append(jax.ShapeDtypeStruct(inverse, jnp.float32))
        sems += [pltpu.SemaphoreType.DMA((2,)), pltpu.SemaphoreType.DMA]
        sems += [pltpu.SemaphoreType.DMA((4,))] * 5
    return pl.pallas_call(
        functools.partial(exchange_body, count, bool(weights)),
        out_shape=out_shape,
        in_specs=[VMEM] * (2 + len(weights)) + [SMEM, VMEM, VMEM][: len(edges)],
        out_specs=[ANY] * len(out_shape),
        scratch_shapes=scratch + sems,
        compiler_params=pltpu.CompilerParams(
            collective_id=0 if weights else 1,
            has_side_effects=True,
            vmem_limit_bytes=LIMIT,
        ),
        name="exchange_weights" if weights else "exchange",
    )(turned, rows, *weights, *edges)


def layer_body(
    relu,
    layer,
    count_ref,
    source_ref,
    target_ref,
    relation_ref,
    own_hbm,
    recv_hbm,
    weight_hbm,
    inverse_hbm,
    bias_ref,
    out_ref,
    table,
    pooled,
    inverse_ref,
    stage_a,
    stage_b,
    own_ref,
    recv_ref,
    weight_ref,
    doubled,
    window_row,
    window_ref,
    ids_0,
    ids_1,
    own_sem,
    recv_sem,
    weight_sem,
    inverse_sem,
    window_sem,
    ids_sem,
):
    nodes, width = own_ref.shape
    relations = weight_ref.shape[0] - 1
    blocks, block_width = target_ref.shape
    slots = WIN * relations
    chunk = 256
    pieces = recv_sem.shape[0]
    piece = recv_ref.shape[0] // pieces

    own_copy = pltpu.make_async_copy(own_hbm, own_ref, own_sem)
    own_copy.start()
    recv_copies = []
    for p in range(pieces):
        rows = pl.ds(p * piece, piece)
        copy = pltpu.make_async_copy(recv_hbm.at[rows], recv_ref.at[rows], recv_sem.at[p])
        copy.start()
        recv_copies.append(copy)
    weight_copy = pltpu.make_async_copy(weight_hbm.at[layer], weight_ref, weight_sem)
    weight_copy.start()
    inverse_copy = pltpu.make_async_copy(inverse_hbm, inverse_ref, inverse_sem)
    inverse_copy.start()

    rows_per_chunk = ids_0.shape[0]
    chunks = blocks // rows_per_chunk
    doubled[...] = source_ref[...] * 2
    first = target_ref[...].T
    window_row[...] = lax.shift_right_logical(first[:8, :], 4)

    def clear(i, carry):
        at = pl.multiple_of(i * slots, slots)
        pooled[pl.ds(at, slots), :] = jnp.zeros((slots, width), jnp.float32)
        return carry

    lax.fori_loop(0, nodes // WIN, clear, 0)
    stage_b[...] = jnp.zeros_like(stage_b)

    ids = (ids_0, ids_1)

    def fetch(chunk, j):
        first_row = pl.multiple_of(
            jnp.minimum(chunk, chunks - 1) * rows_per_chunk, rows_per_chunk
        )
        return pltpu.make_async_copy(
            doubled.at[pl.ds(first_row, rows_per_chunk)], ids[j], ids_sem.at[j]
        )

    window_copy = pltpu.make_async_copy(window_row, window_ref, window_sem)
    window_copy.start()
    for j in range(len(ids)):
        fetch(j, j).start()

    def fill(src_ref, first, last, base):
        def step(i, carry):
            rows = src_ref[pl.ds(pl.multiple_of(i * chunk, chunk), chunk), :].astype(jnp.float32)
            at = pl.multiple_of(base + i * 2 * chunk, 2 * chunk)
            table[pl.ds(at, chunk, stride=2), :] = rows[:, :LANES]
            table[pl.ds(at + 1, chunk, stride=2), :] = rows[:, LANES:]
            return carry

        lax.fori_loop(first, last, step, 0)

    own_copy.wait()
    fill(own_ref, 0, nodes // chunk, 0)
    for p in range(pieces):
        recv_copies[p].wait()
        fill(recv_ref, p * piece // chunk, (p + 1) * piece // chunk, 2 * nodes)

    used = count_ref[0]

    def gather(id_ref, first_row, stage):
        for h in range(2):
            for e in range(block_width):
                at = pl.multiple_of(id_ref[first_row + h, e], 2)
                stage[pl.ds(2 * (h * block_width + e), 2), :] = table[pl.ds(at, 2), :]

    def pool(pair, stage):
        known = jnp.maximum(pair, 0)
        slot = []
        for h in range(2):
            row = pl.ds(2 * known + h, 1)
            in_use = jnp.logical_and(pair >= 0, 2 * pair + h < used)
            shift = jnp.where(in_use, h * slots, 2 * slots)
            slot.append(
                relation_ref[row, :] * WIN + lax.bitwise_and(target_ref[row, :], WIN - 1) + shift
            )
        both = jnp.concatenate(slot, axis=1)
        hot = (
            both == lax.broadcasted_iota(jnp.int32, (2 * slots, 2 * block_width), 0)
        ).astype(jnp.float32).astype(jnp.bfloat16)
        edges = 2 * block_width
        data = jnp.concatenate(
            [
                stage[pl.ds(0, edges, stride=2), :].astype(jnp.bfloat16),
                stage[pl.ds(1, edges, stride=2), :].astype(jnp.bfloat16),
            ],
            axis=1,
        )
        got = jnp.dot(hot, data, preferred_element_type=jnp.float32)
        for h in range(2):
            at = pl.multiple_of(window_ref[0, 2 * known + h] * slots, slots)
            rows = pl.ds(at, slots)
            pooled[rows, :] += got[h * slots : (h + 1) * slots]

    pairs_per_step = len(ids) * rows_per_chunk // 2
    stages = (stage_a, stage_b)
    window_copy.wait()

    def step(i, carry):
        for j in range(len(ids)):
            fetch(0, j).wait()
            for k in range(rows_per_chunk // 2):
                n = j * rows_per_chunk // 2 + k
                pool(i * pairs_per_step + n - 1, stages[(n + 1) % 2])
                gather(ids[j], 2 * k, stages[n % 2])
            fetch((i + 1) * len(ids) + j, j).start()
        return carry

    steps = (used + 2 * pairs_per_step - 1) // (2 * pairs_per_step)
    lax.fori_loop(0, steps, step, 0)
    pool(steps * pairs_per_step - 1, stage_b)
    for j in range(len(ids)):
        fetch(0, j).wait()

    weight_copy.wait()
    inverse_copy.wait()
    part = 256
    windows = part // WIN

    def finish(i, carry):
        at = pl.multiple_of(i * part, part)
        own = own_ref[pl.ds(at, part), :]

        def weight(r):
            return jnp.concatenate([weight_ref[r, 0], weight_ref[r, 1]], axis=1)

        total = bias_ref[...] + jnp.dot(
            own, weight(relations), preferred_element_type=jnp.float32
        )
        base = pl.multiple_of(i * windows * slots, windows * slots)
        sums = pooled[pl.ds(base, windows * slots), :].reshape(windows, relations, WIN, width)
        scale = inverse_ref[pl.ds(base, windows * slots), :].reshape(
            windows, relations, WIN, LANES
        )
        for r in range(relations):
            inverse = scale[:, r].reshape(part, LANES)
            sums_r = sums[:, r].reshape(part, width)
            mean = jnp.concatenate(
                [sums_r[:, :LANES] * inverse, sums_r[:, LANES:] * inverse], axis=1
            ).astype(jnp.bfloat16)
            total = total + jnp.dot(mean, weight(r), preferred_element_type=jnp.float32)
        if relu:
            total = jnp.maximum(total, 0.0)
        out_ref[pl.ds(at, part), :] = total.astype(jnp.bfloat16)
        return carry

    lax.fori_loop(0, nodes // part, finish, 0)


def relational_layer(
    layer, rows, received, count, sources, targets, relation_ids, weights, inverse, bias
):
    nodes, width = rows.shape
    relations = weights.shape[1] - 1
    table_rows = 2 * (nodes + received.shape[0])
    pieces = 4
    return pl.pallas_call(
        functools.partial(layer_body, layer == 0, layer),
        out_shape=jax.ShapeDtypeStruct((nodes, width), jnp.bfloat16),
        in_specs=[SMEM, VMEM, VMEM, VMEM, ANY, ANY, ANY, ANY, VMEM],
        out_specs=VMEM,
        scratch_shapes=[
            pltpu.VMEM((table_rows, LANES), jnp.float32),
            pltpu.VMEM((nodes * relations, width), jnp.float32),
            pltpu.VMEM((nodes * relations, LANES), jnp.float32),
            pltpu.VMEM((4 * LANES, LANES), jnp.float32),
            pltpu.VMEM((4 * LANES, LANES), jnp.float32),
            pltpu.VMEM(rows.shape, rows.dtype),
            pltpu.VMEM(received.shape, received.dtype),
            pltpu.VMEM(weights.shape[1:], weights.dtype),
            pltpu.VMEM(sources.shape, sources.dtype),
            pltpu.VMEM((8, LANES), sources.dtype),
            pltpu.SMEM((8, LANES), sources.dtype),
            pltpu.SMEM((CHUNK_BLOCKS, LANES), sources.dtype),
            pltpu.SMEM((CHUNK_BLOCKS, LANES), sources.dtype),
            pltpu.SemaphoreType.DMA,
            pltpu.SemaphoreType.DMA((pieces,)),
            pltpu.SemaphoreType.DMA,
            pltpu.SemaphoreType.DMA,
            pltpu.SemaphoreType.DMA,
            pltpu.SemaphoreType.DMA((2,)),
        ],
        compiler_params=pltpu.CompilerParams(
            vmem_limit_bytes=LIMIT,
        ),
        name="relational_layer",
    )(
        count, sources, targets, relation_ids, rows, received, weights, inverse,
        bias.reshape(1, width),
    )


def shards(
    features,
    edge_source,
    edge_relation,
    edge_target,
    block_count,
    send_list,
    bases_first,
    self_first,
    coef_first,
    bias_first,
    bases_second,
    self_second,
    coef_second,
    bias_second,
):
    edges = (block_count, edge_source[0], edge_target[0], edge_relation[0])
    turned = jnp.swapaxes(send_list[0], 0, 1)
    width = features.shape[1]
    received, full, inverse = exchange(
        turned,
        features,
        (coef_first, bases_first, self_first, coef_second, bases_second, self_second),
        (block_count, edge_target[0], edge_relation[0]),
    )
    full = full.reshape(full.shape[:3] + (width, LANES))
    hidden = relational_layer(
        0, features, received.reshape(-1, width), *edges, full, inverse, bias_first
    )
    (received,) = exchange(turned, hidden)
    return relational_layer(
        1, hidden, received.reshape(-1, width), *edges, full, inverse, bias_second
    )


def solution(mesh):
    placed = (
        P("dom", None),
        P("dom", None, None),
        P("dom", None, None),
        P("dom", None, None),
        P("dom"),
        P("dom", None, None),
        P(None, "dom", None),
        P("dom", None),
        P(),
        P(),
        P(None, "dom", None),
        P("dom", None),
        P(),
        P(),
    )
    return jax.shard_map(
        shards, mesh=mesh, in_specs=placed, out_specs=P("dom", None), check_vma=False
    )
```

profile of v0, /device:TPU:2, one launch (start us, length us, event | category | flops | bytes accessed | tf_op | source)
XLA Modules:
  0.0 125.6 jit_solution(11668810801748083039)
XLA Ops:
  0.7 46.2 %exchange_weights.1 = (bf16[128,32,256]{2,1,0:T(8,128)(2,1)}, bf16[2,9,2,4,4,8,2,128]{7,6,5,4,3,2,1,0:T(2,128)(2,1)}, f32[8192,128]{1,0:T(8,128)}) custom-call(s32[32,128]{1,0:T(8,128)} %bitcast.23, bf16[1024,256]{1,0:T(8,128)(2,1)} %own_hbm.1, f32[8,30]{1,0:T(8,128)} %refs_2_.1, bf16[30,2,256]{2,1,0:T(2,128)(2,1)} %refs_3_.1, bf16[2,256]{1,0:T(2,128)(2,1)} %refs_4_.1, ...), custom_call_target="tpu_custom_call" | custom-call | tf_op jit(solution)/shard_map/exchange_weights/pallas_call | solution.py:285
  46.9 21.3 %relational_layer.2.refs_1_.own_hbm = bf16[1024,256]{1,0:T(8,128)(2,1)} custom-call(s32[1]{0:T(128)S(6)} %copy.15.refs_8_.count_ref, s32[128,128]{1,0:T(8,128)} %bitcast.21, s32[128,128]{1,0:T(8,128)} %bitcast.16, s32[128,128]{1,0:T(8,128)} %bitcast.19, bf16[1024,256]{1,0:T(8,128)(2,1)} %own_hbm.1, bf16[4096,256]{1,0:T(8,128)(2,1)} %bitcast.14, ...), custom_call_target="tpu_custom_call" | custom-call | tf_op jit(solution)/shard_map/relational_layer/pallas_call | solution.py:497
  68.2 36.1 %exchange.1 = bf16[128,32,256]{2,1,0:T(8,128)(2,1)} custom-call(s32[32,128]{1,0:T(8,128)} %bitcast.24, bf16[1024,256]{1,0:T(8,128)(2,1)} %relational_layer.2.refs_1_.own_hbm), custom_call_target="tpu_custom_call" | custom-call | tf_op jit(solution)/shard_map/exchange/pallas_call | solution.py:285
  104.3 21.3 %relational_layer.3 = bf16[1024,256]{1,0:T(8,128)(2,1)} custom-call(s32[1]{0:T(128)S(6)} %copy.15.refs_8_.count_ref, s32[128,128]{1,0:T(8,128)} %bitcast.22, s32[128,128]{1,0:T(8,128)} %bitcast.17, s32[128,128]{1,0:T(8,128)} %bitcast.20, bf16[1024,256]{1,0:T(8,128)(2,1)} %relational_layer.2.refs_1_.own_hbm, bf16[4096,256]{1,0:T(8,128)(2,1)} %bitcast.13, ...), custom_call_target="tpu_custom_call" | custom-call | tf_op jit(solution)/shard_map/relational_layer/pallas_call | solution.py:497
where the time goes:
time: 126 us
  Pallas kernels  125 us (99%)
    pallas_call x2, Pallas kernels, exchange(): pl.pallas_call(functools.partial(exchange_body, count, bool(weights)), ou...  82.3 us
    pallas_call x2, Pallas kernels, relational_layer(): pl.pallas_call(functools.partial(layer_body, layer == 0, layer), out_shap...  42.6 us

commit v1 on v0

--- a/solution.py
+++ b/solution.py
@@ -39,7 +39,7 @@
 ANY = pl.BlockSpec(memory_space=pl.ANY)
 GROUP = 8
 FIRST_GROUPS = 6
-CHUNK_BLOCKS = 8
+CHUNK_BLOCKS = 16
 
 
 def rows_of_group(group, send_ref, rows_ref, out_ref):
@@ -116,13 +116,20 @@
 
 def exchange_body(count, with_weights, *refs):
     if with_weights:
+        inputs, count_ref, refs = refs[:10], refs[10], refs[11:]
+        (in_ref, full_ref, inverse_out, out_ref, send_ref, part_ref, tally_ref, inverse_ref,
+         send_sem, recv_sem, plane_send, plane_recv, far_send, far_recv, core_send, core_recv,
+         inverse_sem), refs = refs[:17], refs[17:]
         (turned_ref, rows_ref, coef_a, bases_a, self_a, coef_b, bases_b, self_b,
-         count_ref, target_ref, relation_ref,
-         in_ref, full_ref, inverse_out, out_ref, send_ref, part_ref, tally_ref, inverse_ref,
-         send_sem, recv_sem, plane_send, plane_recv, far_send, far_recv, core_send, core_recv,
-         inverse_sem) = refs
+         target_ref, relation_ref) = refs[:10]
     else:
-        turned_ref, rows_ref, in_ref, out_ref, send_ref, send_sem, recv_sem = refs
+        inputs, refs = refs[:2], refs[2:]
+        (in_ref, out_ref, send_ref, send_sem, recv_sem), refs = refs[:5], refs[5:]
+        turned_ref, rows_ref = refs[:2]
+    loads = [
+        pltpu.make_async_copy(src, dst, refs[-1].at[i])
+        for i, (src, dst) in enumerate(zip(inputs, refs[:-1]))
+    ]
     me = lax.axis_index("dom")
     groups = count // GROUP
     barrier = pltpu.get_barrier_semaphore()
@@ -131,6 +138,10 @@
         pl.semaphore_signal(
             barrier, inc=1, device_id=(lax.rem(me + k, count),), device_id_type=MESH
         )
+    for load in loads:
+        load.start()
+    for load in loads:
+        load.wait()
 
     def group_at(t):
         return lax.rem(me // GROUP + 5 * t, groups)
@@ -264,6 +275,7 @@
 
 def exchange(turned, rows, weights=(), edges=()):
     slots, count = turned.shape
+    loaded = (turned, rows, *weights, *edges[1:])
     block = (count, slots, rows.shape[1])
     out_shape = [jax.ShapeDtypeStruct(block, rows.dtype)]
     scratch = [pltpu.VMEM(block, rows.dtype), pltpu.VMEM((count, slots), turned.dtype)]
@@ -285,30 +297,33 @@
     return pl.pallas_call(
         functools.partial(exchange_body, count, bool(weights)),
         out_shape=out_shape,
-        in_specs=[VMEM] * (2 + len(weights)) + [SMEM, VMEM, VMEM][: len(edges)],
+        in_specs=[ANY] * len(loaded) + [SMEM] * len(edges[:1]),
         out_specs=[ANY] * len(out_shape),
-        scratch_shapes=scratch + sems,
+        scratch_shapes=scratch
+        + sems
+        + [pltpu.VMEM(array.shape, array.dtype) for array in loaded]
+        + [pltpu.SemaphoreType.DMA((len(loaded),))],
         compiler_params=pltpu.CompilerParams(
             collective_id=0 if weights else 1,
             has_side_effects=True,
             vmem_limit_bytes=LIMIT,
         ),
         name="exchange_weights" if weights else "exchange",
-    )(turned, rows, *weights, *edges)
+    )(*loaded, *edges[:1])
 
 
 def layer_body(
     relu,
     layer,
     count_ref,
-    source_ref,
-    target_ref,
-    relation_ref,
+    source_hbm,
+    target_hbm,
+    relation_hbm,
     own_hbm,
     recv_hbm,
     weight_hbm,
     inverse_hbm,
-    bias_ref,
+    bias_hbm,
     out_ref,
     table,
     pooled,
@@ -329,6 +344,11 @@
     inverse_sem,
     window_sem,
     ids_sem,
+    source_ref,
+    target_ref,
+    relation_ref,
+    bias_ref,
+    small_sem,
 ):
     nodes, width = own_ref.shape
     relations = weight_ref.shape[0] - 1
@@ -338,6 +358,19 @@
     pieces = recv_sem.shape[0]
     piece = recv_ref.shape[0] // pieces
 
+    small = [
+        pltpu.make_async_copy(src, dst, small_sem.at[i])
+        for i, (src, dst) in enumerate(
+            [
+                (source_hbm, source_ref),
+                (target_hbm, target_ref),
+                (relation_hbm, relation_ref),
+                (bias_hbm, bias_ref),
+            ]
+        )
+    ]
+    for copy in small:
+        copy.start()
     own_copy = pltpu.make_async_copy(own_hbm, own_ref, own_sem)
     own_copy.start()
     recv_copies = []
@@ -347,9 +380,9 @@
         copy.start()
         recv_copies.append(copy)
     weight_copy = pltpu.make_async_copy(weight_hbm.at[layer], weight_ref, weight_sem)
-    weight_copy.start()
     inverse_copy = pltpu.make_async_copy(inverse_hbm, inverse_ref, inverse_sem)
-    inverse_copy.start()
+    for copy in small:
+        copy.wait()
 
     rows_per_chunk = ids_0.shape[0]
     chunks = blocks // rows_per_chunk
@@ -395,6 +428,8 @@
     for p in range(pieces):
         recv_copies[p].wait()
         fill(recv_ref, p * piece // chunk, (p + 1) * piece // chunk, 2 * nodes)
+    weight_copy.start()
+    inverse_copy.start()
 
     used = count_ref[0]
 
@@ -497,7 +532,7 @@
     return pl.pallas_call(
         functools.partial(layer_body, layer == 0, layer),
         out_shape=jax.ShapeDtypeStruct((nodes, width), jnp.bfloat16),
-        in_specs=[SMEM, VMEM, VMEM, VMEM, ANY, ANY, ANY, ANY, VMEM],
+        in_specs=[SMEM] + [ANY] * 8,
         out_specs=VMEM,
         scratch_shapes=[
             pltpu.VMEM((table_rows, LANES), jnp.float32),
@@ -519,6 +554,11 @@
             pltpu.SemaphoreType.DMA,
             pltpu.SemaphoreType.DMA,
             pltpu.SemaphoreType.DMA((2,)),
+            pltpu.VMEM(sources.shape, sources.dtype),
+            pltpu.VMEM(sources.shape, sources.dtype),
+            pltpu.VMEM(sources.shape, sources.dtype),
+            pltpu.VMEM((1, width), jnp.float32),
+            pltpu.SemaphoreType.DMA((4,)),
         ],
         compiler_params=pltpu.CompilerParams(
             vmem_limit_bytes=LIMIT,

time: 126 us -> 122 us (0.968)
  Pallas kernels: 125 us -> 121 us
    pallas_call x2, Pallas kernels: 82.3 us -> 80.3 us  [exchange(): pl.pallas_call(functools.partial(exchange_body, count, bool(weights)), ou...]
    pallas_call x2, Pallas kernels: 42.6 us -> 40.9 us  [relational_layer(): pl.pallas_call(functools.partial(layer_body, layer == 0, layer), out_shap...]
where the time goes in v1:
time: 122 us
  Pallas kernels  121 us (99%)
    pallas_call x2, Pallas kernels, exchange(): pl.pallas_call(functools.partial(exchange_body, count, bool(weights)), ou...  80.3 us
    pallas_call x2, Pallas kernels, relational_layer(): pl.pallas_call(functools.partial(layer_body, layer == 0, layer), out_shap...  40.9 us

profile of v1, /device:TPU:2, one launch (start us, length us, event | category | flops | bytes accessed | tf_op | source)
XLA Modules:
  0.0 121.9 jit_solution(3438825442439691507)
XLA Ops:
  0.7 45.3 %exchange_weights.1 = (bf16[128,32,256]{2,1,0:T(8,128)(2,1)}, bf16[2,9,2,4,4,8,2,128]{7,6,5,4,3,2,1,0:T(2,128)(2,1)}, f32[8192,128]{1,0:T(8,128)}) custom-call(s32[32,128]{1,0:T(8,128)} %bitcast.23, bf16[1024,256]{1,0:T(8,128)(2,1)} %own_hbm.1, f32[8,30]{1,0:T(8,128)} %refs_2_.1, bf16[30,2,256]{2,1,0:T(2,128)(2,1)} %refs_3_.1, bf16[2,256]{1,0:T(2,128)(2,1)} %refs_4_.1, ...), custom_call_target="tpu_custom_call" | custom-call | tf_op jit(solution)/shard_map/exchange_weights/pallas_call | solution.py:297
  46.0 20.5 %relational_layer.2.refs_1_.own_hbm = bf16[1024,256]{1,0:T(8,128)(2,1)} custom-call(s32[1]{0:T(128)S(6)} %copy.15.refs_10_.count_ref, s32[128,128]{1,0:T(8,128)} %bitcast.21, s32[128,128]{1,0:T(8,128)} %bitcast.16, s32[128,128]{1,0:T(8,128)} %bitcast.19, bf16[1024,256]{1,0:T(8,128)(2,1)} %own_hbm.1, bf16[4096,256]{1,0:T(8,128)(2,1)} %bitcast.14, ...), custom_call_target="tpu_custom_call" | custom-call | tf_op jit(solution)/shard_map/relational_layer/pallas_call | solution.py:532
  66.4 35.0 %exchange.1 = bf16[128,32,256]{2,1,0:T(8,128)(2,1)} custom-call(s32[32,128]{1,0:T(8,128)} %bitcast.24, bf16[1024,256]{1,0:T(8,128)(2,1)} %relational_layer.2.refs_1_.own_hbm), custom_call_target="tpu_custom_call" | custom-call | tf_op jit(solution)/shard_map/exchange/pallas_call | solution.py:297
  101.4 20.4 %relational_layer.3 = bf16[1024,256]{1,0:T(8,128)(2,1)} custom-call(s32[1]{0:T(128)S(6)} %copy.15.refs_10_.count_ref, s32[128,128]{1,0:T(8,128)} %bitcast.22, s32[128,128]{1,0:T(8,128)} %bitcast.17, s32[128,128]{1,0:T(8,128)} %bitcast.20, bf16[1024,256]{1,0:T(8,128)(2,1)} %relational_layer.2.refs_1_.own_hbm, bf16[4096,256]{1,0:T(8,128)(2,1)} %bitcast.13, ...), custom_call_target="tpu_custom_call" | custom-call | tf_op jit(solution)/shard_map/relational_layer/pallas_call | solution.py:532

commit v2 on v1

--- a/solution.py
+++ b/solution.py
@@ -324,7 +324,7 @@
     weight_hbm,
     inverse_hbm,
     bias_hbm,
-    out_ref,
+    out_hbm,
     table,
     pooled,
     inverse_ref,
@@ -349,6 +349,8 @@
     relation_ref,
     bias_ref,
     small_sem,
+    out_ref,
+    out_sem,
 ):
     nodes, width = own_ref.shape
     relations = weight_ref.shape[0] - 1
@@ -492,6 +494,10 @@
     part = 256
     windows = part // WIN
 
+    def put(i):
+        rows = pl.ds(pl.multiple_of(i * part, part), part)
+        return pltpu.make_async_copy(out_ref.at[rows], out_hbm.at[rows], out_sem.at[i])
+
     def finish(i, carry):
         at = pl.multiple_of(i * part, part)
         own = own_ref[pl.ds(at, part), :]
@@ -517,9 +523,18 @@
         if relu:
             total = jnp.maximum(total, 0.0)
         out_ref[pl.ds(at, part), :] = total.astype(jnp.bfloat16)
+
+        @pl.when(i > 0)
+        def _():
+            put(i - 1).start()
+
         return carry
 
-    lax.fori_loop(0, nodes // part, finish, 0)
+    parts = nodes // part
+    lax.fori_loop(0, parts, finish, 0)
+    put(parts - 1).start()
+    for i in range(parts):
+        put(i).wait()
 
 
 def relational_layer(
@@ -533,7 +548,7 @@
         functools.partial(layer_body, layer == 0, layer),
         out_shape=jax.ShapeDtypeStruct((nodes, width), jnp.bfloat16),
         in_specs=[SMEM] + [ANY] * 8,
-        out_specs=VMEM,
+        out_specs=ANY,
         scratch_shapes=[
             pltpu.VMEM((table_rows, LANES), jnp.float32),
             pltpu.VMEM((nodes * relations, width), jnp.float32),
@@ -559,6 +574,8 @@
             pltpu.VMEM(sources.shape, sources.dtype),
             pltpu.VMEM((1, width), jnp.float32),
             pltpu.SemaphoreType.DMA((4,)),
+            pltpu.VMEM((nodes, width), jnp.bfloat16),
+            pltpu.SemaphoreType.DMA((4,)),
         ],
         compiler_params=pltpu.CompilerParams(
             vmem_limit_bytes=LIMIT,

time: 122 us -> 123 us (level)
  no operation moved by 1% of the time
where the time goes in v2:
time: 123 us; the launch traced here: 122 us
  Pallas kernels  121 us (98%)
    pallas_call x2, Pallas kernels, exchange(): pl.pallas_call(functools.partial(exchange_body, count, bool(weights)), ou...  80.2 us
    pallas_call x2, Pallas kernels, relational_layer(): pl.pallas_call(functools.partial(layer_body, layer == 0, layer), out_shap...  40.8 us

profile of v2, /device:TPU:2, one launch (start us, length us, event | category | flops | bytes accessed | tf_op | source)
XLA Modules:
  0.0 121.7 jit_solution(9443299257989401673)
XLA Ops:
  0.7 45.3 %exchange_weights.1 = (bf16[128,32,256]{2,1,0:T(8,128)(2,1)}, bf16[2,9,2,4,4,8,2,128]{7,6,5,4,3,2,1,0:T(2,128)(2,1)}, f32[8192,128]{1,0:T(8,128)}) custom-call(s32[32,128]{1,0:T(8,128)} %bitcast.23, bf16[1024,256]{1,0:T(8,128)(2,1)} %own_hbm.1, f32[8,30]{1,0:T(8,128)} %refs_2_.1, bf16[30,2,256]{2,1,0:T(2,128)(2,1)} %refs_3_.1, bf16[2,256]{1,0:T(2,128)(2,1)} %refs_4_.1, ...), custom_call_target="tpu_custom_call" | custom-call | tf_op jit(solution)/shard_map/exchange_weights/pallas_call | solution.py:297
  46.0 20.4 %relational_layer.2.refs_1_.own_hbm = bf16[1024,256]{1,0:T(8,128)(2,1)} custom-call(s32[1]{0:T(128)S(6)} %copy.15.refs_10_.count_ref, s32[128,128]{1,0:T(8,128)} %bitcast.21, s32[128,128]{1,0:T(8,128)} %bitcast.16, s32[128,128]{1,0:T(8,128)} %bitcast.19, bf16[1024,256]{1,0:T(8,128)(2,1)} %own_hbm.1, bf16[4096,256]{1,0:T(8,128)(2,1)} %bitcast.14, ...), custom_call_target="tpu_custom_call" | custom-call | tf_op jit(solution)/shard_map/relational_layer/pallas_call | solution.py:547
  66.4 34.9 %exchange.1 = bf16[128,32,256]{2,1,0:T(8,128)(2,1)} custom-call(s32[32,128]{1,0:T(8,128)} %bitcast.24, bf16[1024,256]{1,0:T(8,128)(2,1)} %relational_layer.2.refs_1_.own_hbm), custom_call_target="tpu_custom_call" | custom-call | tf_op jit(solution)/shard_map/exchange/pallas_call | solution.py:297
  101.3 20.4 %relational_layer.3 = bf16[1024,256]{1,0:T(8,128)(2,1)} custom-call(s32[1]{0:T(128)S(6)} %copy.15.refs_10_.count_ref, s32[128,128]{1,0:T(8,128)} %bitcast.22, s32[128,128]{1,0:T(8,128)} %bitcast.17, s32[128,128]{1,0:T(8,128)} %bitcast.20, bf16[1024,256]{1,0:T(8,128)(2,1)} %relational_layer.2.refs_1_.own_hbm, bf16[4096,256]{1,0:T(8,128)(2,1)} %bitcast.13, ...), custom_call_target="tpu_custom_call" | custom-call | tf_op jit(solution)/shard_map/relational_layer/pallas_call | solution.py:547
